TPU v7x, 128 devices: a whole 4x4x4 slice. The times are simulated.
128 devices in a mesh: ctx: 32 (over y, z, core), head: 4 (over x).
Axes of the slice: x: 4, y: 4, z: 4, core: 2. Of those that a mesh axis runs over, the one named last changes fastest.
Arguments:
- query: bfloat16 [65536, 2048], P('ctx', 'head'), may hold values from -6 to 6
- key: bfloat16 [65536, 2048], P('ctx', 'head'), may hold values from -6 to 6
- value: bfloat16 [65536, 2048], P('ctx', 'head'), may hold values from -6 to 6
- gain: bfloat16 [2048], P('head'), may hold values from 0.099609375 to 1.8984375
- w_out: bfloat16 [2048, 2048], replicated, may hold values from -0.125 to 0.125
- d_out: bfloat16 [65536, 2048], P(('ctx', 'head')), may hold values from -6 to 6
Outputs:
- out: bfloat16 [65536, 2048], P(('ctx', 'head'))
- grad_query: bfloat16 [65536, 2048], P('ctx', 'head')
- grad_key: bfloat16 [65536, 2048], P('ctx', 'head')
- grad_value: bfloat16 [65536, 2048], P('ctx', 'head')
All inputs are finite; a program needn't handle non-finite values.
Results may differ from a plain program's by a relative error of at most 0.018.
Values may be sent and summed in bfloat16 or wider, within the bound.
A program may use at most 128 MiB of HBM per device.

v0:
```python
import jax
import jax.numpy as jnp
from jax import lax
from jax.sharding import Mesh
from jax.sharding import PartitionSpec as P

HDIM = 128
BLOCK = 128
CTX = ("ctx_0", "ctx_1", "ctx_2")
CTX_HEAD = ("ctx_0", "ctx_1", "ctx_2", "head")
epsilon = 1e-06


def nothing_yet(value, identity):
    return jnp.broadcast_to(jnp.asarray(identity, value.dtype), value.shape)


def prefix_by_axis(value, axes, combine, identity, reverse):
    before = start = nothing_yet(value, identity)
    total = value
    for axis in reversed(axes):
        length, mine = (lax.axis_size(axis), lax.axis_index(axis))
        pieces = lax.all_gather(total.astype(jnp.bfloat16), axis)
        inside, total = (start, start)
        for k in reversed(range(length)) if reverse else range(length):
            passed = k > mine if reverse else k < mine
            total = combine(total, pieces[k].astype(value.dtype))
            inside = jnp.where(passed, total, inside)
        before = combine(inside, before)
    return before


def add_states(earlier, later):
    return earlier + later


def earlier_states(local_total):
    return prefix_by_axis(local_total, CTX, add_states, jnp.zeros_like(local_total), False)


def later_states(local_total):
    return prefix_by_axis(local_total, CTX, add_states, jnp.zeros_like(local_total), True)


def on_device(query, key, value, gain, w_out, d_out):
    tokens, width = query.shape
    local_heads = width // HDIM
    nblocks = tokens // BLOCK
    causal = jnp.tril(jnp.ones((BLOCK, BLOCK), dtype=bool))[None, None]

    def split_blocks(array):
        return array.reshape(nblocks, BLOCK, local_heads, HDIM)

    def masked(scores):
        return jnp.where(causal, scores, jnp.zeros_like(scores)).astype(jnp.bfloat16)

    q_blocks = split_blocks(query)
    k_blocks = split_blocks(key)
    v_blocks = split_blocks(value)
    scores = masked(
        jnp.einsum("cshe,cthe->chst", q_blocks, k_blocks, preferred_element_type=jnp.float32)
    )
    block_states = jnp.einsum(
        "cshe,cshf->chef", k_blocks, v_blocks, preferred_element_type=jnp.float32
    )
    before = earlier_states(jnp.sum(block_states, axis=0))
    running = jnp.cumsum(block_states, axis=0)
    inner_before = jnp.concatenate([jnp.zeros_like(running[:1]), running[:-1]], axis=0)
    prefixes = (before[None] + inner_before).astype(jnp.bfloat16)
    attended = jnp.einsum("chst,cthf->cshf", scores, v_blocks, preferred_element_type=jnp.float32)
    attended = attended + jnp.einsum(
        "cshe,chef->cshf", q_blocks, prefixes, preferred_element_type=jnp.float32
    )
    attended = attended.reshape(tokens, local_heads, HDIM)
    inverse = lax.rsqrt(jnp.mean(attended * attended, axis=-1, keepdims=True) + epsilon)
    unit = attended * inverse
    scales = gain.astype(jnp.float32).reshape(local_heads, HDIM)
    normed = (unit * scales).astype(jnp.bfloat16).reshape(tokens, width)
    w_slice = lax.dynamic_slice_in_dim(w_out, lax.axis_index("head") * width, width, 0)
    out = lax.psum_scatter(
        jnp.dot(normed, w_slice, preferred_element_type=jnp.float32).astype(jnp.bfloat16),
        "head",
        scatter_dimension=0,
        tiled=True,
    )
    grad_heads = lax.dot_general(
        lax.all_gather(d_out, "head", axis=0, tiled=True),
        w_slice,
        (((1,), (1,)), ((), ())),
        preferred_element_type=jnp.float32,
    ).astype(jnp.bfloat16)
    grad_unit = grad_heads.astype(jnp.float32).reshape(tokens, local_heads, HDIM) * scales
    grad_attended = inverse * (
        grad_unit - unit * jnp.mean(grad_unit * unit, axis=-1, keepdims=True)
    )
    g_blocks = split_blocks(grad_attended.astype(jnp.bfloat16))
    grad_scores = masked(
        jnp.einsum("cshf,cthf->chst", g_blocks, v_blocks, preferred_element_type=jnp.float32)
    )
    block_grads = jnp.einsum(
        "cshe,cshf->chef", q_blocks, g_blocks, preferred_element_type=jnp.float32
    )
    after = later_states(jnp.sum(block_grads, axis=0))
    tail_sums = jnp.cumsum(block_grads[::-1], axis=0)[::-1]
    inner_after = jnp.concatenate([tail_sums[1:], jnp.zeros_like(tail_sums[:1])], axis=0)
    suffixes = (after[None] + inner_after).astype(jnp.bfloat16)
    grad_query = jnp.einsum(
        "chst,cthe->cshe", grad_scores, k_blocks, preferred_element_type=jnp.float32
    )
    grad_query = grad_query + jnp.einsum(
        "cshf,chef->cshe", g_blocks, prefixes, preferred_element_type=jnp.float32
    )
    grad_key = jnp.einsum(
        "chst,cshe->cthe", grad_scores, q_blocks, preferred_element_type=jnp.float32
    )
    grad_key = grad_key + jnp.einsum(
        "cthf,chef->cthe", v_blocks, suffixes, preferred_element_type=jnp.float32
    )
    grad_value = jnp.einsum("chst,cshf->cthf", scores, g_blocks, preferred_element_type=jnp.float32)
    grad_value = grad_value + jnp.einsum(
        "cthe,chef->cthf", k_blocks, suffixes, preferred_element_type=jnp.float32
    )
    return (
        out,
        grad_query.reshape(tokens, width).astype(jnp.bfloat16),
        grad_key.reshape(tokens, width).astype(jnp.bfloat16),
        grad_value.reshape(tokens, width).astype(jnp.bfloat16),
    )


def solution(mesh):
    finer = Mesh(
        mesh.devices.reshape(4, 4, 2, mesh.shape["head"]), ("ctx_0", "ctx_1", "ctx_2", "head")
    )
    in_specs = (P(CTX, "head"), P(CTX, "head"), P(CTX, "head"), P("head"), P(), P(CTX_HEAD, None))
    out_specs = (P(CTX_HEAD, None), P(CTX, "head"), P(CTX, "head"), P(CTX, "head"))
    return jax.shard_map(
        on_device, mesh=finer, in_specs=in_specs, out_specs=out_specs, check_vma=False
    )
```

profile of v0, /device:TPU:0, one launch (start us, length us, event | category | flops | bytes accessed | tf_op | source)
XLA Modules:
  0.0 214.9 jit_solution(12444934481127085550)
XLA Ops:
  8.0 2.6 %reshape.94 = bf16[16,128,4,128]{3,2,1,0:T(4,128)(2,1)S(1)} reshape(bf16[2048,512]{1,0:T(8,128)(2,1)} %param.6) | data formatting | bytes 4194304 | tf_op jit(solution)/shard_map/reshape | solution.py:52
  10.5 4.0 %reshape.95 = bf16[16,128,4,128]{3,2,1,0:T(4,128)(2,1)} reshape(bf16[2048,512]{1,0:T(8,128)(2,1)} %param.7) | data formatting | bytes 4194304 | tf_op jit(solution)/shard_map/reshape | solution.py:52
  14.5 4.0 %reshape.96 = bf16[16,128,4,128]{3,2,1,0:T(4,128)(2,1)} reshape(bf16[2048,512]{1,0:T(8,128)(2,1)} %param.8) | data formatting | bytes 4194304 | tf_op jit(solution)/shard_map/reshape | solution.py:52
  18.4 3.1 %fusion.61 = (bf16[4,128,128]{2,1,0:T(8,128)(2,1)S(1)}, f32[16,4,128,128]{3,2,1,0:T(8,128)S(1)}) fusion(bf16[16,128,4,128]{3,2,1,0:T(4,128)(2,1)} %reshape.96, bf16[16,128,4,128]{3,2,1,0:T(4,128)(2,1)} %reshape.95), kind=kOutput, calls=%fused_computation.99 | convolution fusion | flops 269418496 | bytes 8519680 | tf_op jit(solution)/shard_map/cshe,cshf->chef/dot_general | solution.py:63
  21.6 6.4 %fusion.63 = f32[16,4,128,128]{3,2,1,0:T(8,128)S(1)} fusion(f32[16,4,128,128]{3,2,1,0:T(8,128)S(1)} %get-tuple-element.17), kind=kOutput, calls=%fused_computation.101 | output fusion | flops 15728640 | bytes 8388608 | tf_op jit(solution)/shard_map/jit(cumsum)/reduce_window_sum | solution.py:67
  28.5 2.1 all-gather
  30.7 14.4 %all_gather.28 = bf16[4,4,128,128]{3,2,1,0:T(8,128)(2,1)S(1)} all-gather(bf16[1,4,128,128]{3,2,1,0:T(8,128)(2,1)S(1)} %fusion.52), channel_id=1, replica_groups=mesh['ctx_0'=4,'ctx_1'=4,'ctx_2'=2,'head'=4] {'ctx_1'}, dimensions={0}, use_global_device_ids=true | all-gather | bytes 655360 | tf_op jit(solution)/shard_map/all_gather | solution.py:23
  45.2 13.4 %all_gather.29 = bf16[4,4,128,128]{3,2,1,0:T(8,128)(2,1)S(1)} all-gather(bf16[1,4,128,128]{3,2,1,0:T(8,128)(2,1)S(1)} %fusion.51), channel_id=1, replica_groups=mesh['ctx_0'=4,'ctx_1'=4,'ctx_2'=2,'head'=4] {'ctx_0'}, dimensions={0}, use_global_device_ids=true | all-gather | bytes 655360 | tf_op jit(solution)/shard_map/all_gather | solution.py:23
  62.4 3.5 %multiply_reduce_fusion = (f32[16,128,4]{1,2,0:T(4,128)S(1)}, f32[16,128,4,128]{3,1,2,0:T(8,128)}) fusion(f32[15,4,128,128]{3,2,1,0:T(8,128)S(1)} %slice.106, f32[4,128,128]{2,1,0:T(8,128)S(1)} %fusion.31, bf16[16,128,4,128]{3,2,1,0:T(4,128)(2,1)S(1)} %reshape.94, f32[16,4,128,128]{3,2,1,0:T(8,128)S(1)} %fusion.14), kind=kOutput, calls=%fused_computation.16 | convolution fusion | flops 273670144 | bytes 14712832 | tf_op jit(solution)/shard_map/cshe,chef->cshf/dot_general | solution.py:71
  65.9 5.7 %copy.66 = f32[16,128,4,128]{1,0,3,2:T(8,128)} copy(f32[16,128,4,128]{3,1,2,0:T(8,128)} %get-tuple-element.19) | data formatting | bytes 8388608 | tf_op jit(solution)/shard_map/add | solution.py:71
  71.6 4.0 %fusion.1 = bf16[2048,512]{0,1:T(8,128)(2,1)S(1)} fusion(f32[64,8,16,128]{3,2,1,0:T(8,128)} %bitcast.93, f32[2048,4]{0,1:T(4,128)S(1)} %get-tuple-element.13, f32[512]{0:T(512)S(1)} %get-tuple-element.15), kind=kLoop, calls=%fused_computation.3 | loop fusion | flops 3145728 | bytes 6326272 | tf_op jit(solution)/shard_map/convert_element_type | solution.py:78
  75.6 8.4 %convolution_convert_fusion = bf16[2048,2048]{1,0:T(8,128)(2,1)} fusion(bf16[2048,512]{0,1:T(8,128)(2,1)S(1)} %fusion.1, bf16[2048,2048]{1,0:T(8,128)(2,1)} %param.10, s32[]{:T(128)S(6)} %select_n.175), kind=kOutput, calls=%fused_computation | convolution fusion | flops 4299161600 | bytes 12582916 | tf_op jit(solution)/shard_map/dot_general | solution.py:81
  84.0 4.7 %copy.70 = f32[16,128,4,128]{3,1,0,2:T(8,128)} copy(f32[16,128,4,128]{3,1,2,0:T(8,128)} %get-tuple-element.19) | data formatting | bytes 8388608 | tf_op jit(solution)/shard_map/add | solution.py:71
  88.7 6.5 %all-gather.4.cloned.1.call-done = bf16[2048,2048]{1,0:T(8,128)(2,1)} async-done(((bf16[512,2048]{1,0:T(8,128)(2,1)}), bf16[2048,2048]{1,0:T(8,128)(2,1)}) %all-gather.4.cloned.1.call-update) | async-done | bytes 8388624 | tf_op jit(solution)/shard_map/all_gather | solution.py:87
  95.2 7.6 %fusion.6 = f32[512,2048]{1,0:T(8,128)S(1)} fusion(bf16[2048,2048]{1,0:T(8,128)(2,1)} %all-gather.4.cloned.1.call-done, bf16[2048,2048]{1,0:T(8,128)(2,1)} %param.10, s32[]{:T(128)S(6)} %select_n.175), kind=kOutput, calls=%fused_computation.20 | convolution fusion | flops 4297064448 | bytes 14680068 | tf_op jit(solution)/shard_map/dot_general | solution.py:86
  102.8 3.2 %copy.106 = f32[64,8,16,128]{3,2,1,0:T(8,128)} copy(f32[64,8,16,128]{3,1,2,0:T(8,128)S(1)} %bitcast.94) | data formatting | bytes 8388608
  106.1 5.3 %copy.68 = f32[16,128,4,128]{3,1,2,0:T(8,128)} copy(f32[16,128,4,128]{1,0,3,2:T(8,128)} %bitcast.96) | data formatting | bytes 8388608 | tf_op jit(solution)/shard_map/reshape | solution.py:92
  111.4 5.3 %copy.69 = f32[2048,4,128]{2,0,1:T(8,128)} copy(f32[2048,4,128]{0,2,1:T(8,128)} %bitcast.95) | data formatting | bytes 8388608 | tf_op jit(solution)/shard_map/reshape | solution.py:92
  116.7 4.9 %fusion.5 = f32[2048,4]{0,1:T(4,128)S(1)} fusion(f32[16,128,4,128]{3,1,0,2:T(8,128)} %copy.70, f32[2048,4,128]{2,0,1:T(8,128)} %copy.69, f32[4,128]{1,0:T(4,128)S(1)} %get-tuple-element.14, f32[2048,4]{0,1:T(4,128)S(1)} %get-tuple-element.13), kind=kLoop, calls=%fused_computation.10 | loop fusion | flops 4186112 | bytes 8456192 | tf_op jit(solution)/shard_map/reduce_sum | solution.py:94
  122.8 2.7 %multiply_convert_fusion = bf16[16,128,4,128]{3,1,2,0:T(8,128)(2,1)S(1)} fusion(f32[16,128,4,128]{3,1,2,0:T(8,128)S(1)} %copy-done, f32[16,128,4,128]{3,1,2,0:T(8,128)S(1)} %copy-done.12, f32[16,128,4]{1,2,0:T(4,128)S(1)} %multiply_bitcast_fusion, f32[4,128]{1,0:T(4,128)S(1)} %get-tuple-element.14, f32[16,128,4]{1,2,0:T(4,128)S(1)} %get-tuple-element.12), kind=kLoop, calls=%fused_computation.15 | loop fusion | flops 6291456 | bytes 10553344 | tf_op jit(solution)/shard_map/convert_element_type | solution.py:96
  135.9 2.9 %fusion.62 = (bf16[4,128,128]{1,2,0:T(8,128)(2,1)S(1)}, f32[16,4,128,128]{2,3,1,0:T(8,128)}) fusion(bf16[16,128,4,128]{3,1,2,0:T(8,128)(2,1)S(1)} %multiply_convert_fusion, bf16[16,128,4,128]{3,2,1,0:T(4,128)(2,1)S(1)} %reshape.94), kind=kOutput, calls=%fused_computation.100 | convolution fusion | flops 269418496 | bytes 8519680 | tf_op jit(solution)/shard_map/cshe,cshf->chef/dot_general | solution.py:100
  139.0 4.8 %rev.4 = f32[16,4,128,128]{2,3,1,0:T(8,128)} reverse(f32[16,4,128,128]{2,3,1,0:T(8,128)} %get-tuple-element.21), dimensions={0} | reverse | bytes 8388608 | tf_op jit(solution)/shard_map/rev | solution.py:104
  143.7 5.5 %copy.81 = f32[16,4,128,128]{3,2,1,0:T(8,128)} copy(f32[16,4,128,128]{2,3,1,0:T(8,128)} %rev.4) | data formatting | bytes 8388608 | tf_op jit(solution)/shard_map/rev | solution.py:104
  149.2 2.8 %fusion.64 = f32[16,4,128,128]{3,2,1,0:T(8,128)S(1)} fusion(f32[16,4,128,128]{3,2,1,0:T(8,128)} %copy.81), kind=kOutput, calls=%fused_computation.102 | output fusion | flops 15728640 | bytes 8388608 | tf_op jit(solution)/shard_map/jit(cumsum)/reduce_window_sum | solution.py:104
  152.0 2.3 %slice.117 = f32[15,4,128,128]{3,2,1,0:T(8,128)} slice(f32[16,4,128,128]{3,2,1,0:T(8,128)S(1)} %fusion.64), slice={[0:15], [0:4], [0:128], [0:128]} | slice | bytes 7864320 | tf_op jit(solution)/shard_map/slice | solution.py:105
  154.3 4.5 %slice.91 = f32[15,4,128,128]{3,2,1,0:T(8,128)} reverse(f32[15,4,128,128]{3,2,1,0:T(8,128)} %slice.117), dimensions={0} | reverse | bytes 7864320 | tf_op jit(solution)/shard_map/slice | solution.py:105
  158.8 2.1 all-gather.1
  161.0 13.3 %all_gather.32 = bf16[4,4,128,128]{3,2,1,0:T(8,128)(2,1)S(1)} all-gather(bf16[1,4,128,128]{3,2,1,0:T(8,128)(2,1)S(1)} %fusion.53), channel_id=1, replica_groups=mesh['ctx_0'=4,'ctx_1'=4,'ctx_2'=2,'head'=4] {'ctx_1'}, dimensions={0}, use_global_device_ids=true | all-gather | bytes 655360 | tf_op jit(solution)/shard_map/all_gather | solution.py:23
  174.3 13.8 %all_gather.33 = bf16[4,4,128,128]{3,2,1,0:T(8,128)(2,1)S(1)} all-gather(bf16[1,4,128,128]{3,2,1,0:T(8,128)(2,1)S(1)} %fusion.50), channel_id=1, replica_groups=mesh['ctx_0'=4,'ctx_1'=4,'ctx_2'=2,'head'=4] {'ctx_0'}, dimensions={0}, use_global_device_ids=true | all-gather | bytes 655360 | tf_op jit(solution)/shard_map/all_gather | solution.py:23
  196.6 2.9 %fusion.9 = bf16[16,128,4,128]{1,3,2,0:T(8,128)(2,1)} fusion(f32[16,4,128,128]{3,2,1,0:T(8,128)S(1)} %fusion.65, bf16[16,128,4,128]{3,2,1,0:T(4,128)(2,1)S(1)} %copy-done.6, f32[15,4,128,128]{3,2,1,0:T(8,128)S(1)} %copy-done.3, f32[4,128,128]{2,1,0:T(8,128)S(1)} %fusion.40), kind=kOutput, calls=%fused_computation.27 | convolution fusion | flops 272629760 | bytes 12582912 | tf_op jit(solution)/shard_map/cthe,chef->cthf/dot_general | solution.py:120
  199.5 4.3 %copy.100 = bf16[16,128,4,128]{3,2,1,0:T(4,128)(2,1)} copy(bf16[16,128,4,128]{1,3,2,0:T(8,128)(2,1)} %fusion.9) | data formatting | bytes 4194304
  203.8 4.3 %copy_bitcast_fusion = (bf16[2048,512]{1,0:T(8,128)(2,1)}, bf16[2048,512]{1,0:T(8,128)(2,1)}) fusion(bf16[256,8,4,128]{3,2,1,0:T(4,128)(2,1)} %bitcast.99, bf16[256,8,4,128]{3,2,1,0:T(4,128)(2,1)S(1)} %bitcast.98), kind=kLoop, calls=%fused_computation.22 | loop fusion | bytes 8388608
  (66 shorter events, 25.3 us)
Async XLA Ops:
  7.2 88.0 %all-gather.4.cloned.1.call-start = ((), (), s32[]{:S(2)}) async-start(), calls=%async_computation.2 | async-start | bytes 10485760 | tf_op jit(solution)/shard_map/all_gather | solution.py:87
  7.9 200.2 %reduce-scatter.2.cloned.1.call-start = ((), (), s32[]{:S(2)}) async-start(), calls=%async_computation.1 | async-start | bytes 10485760 | tf_op jit(solution)/shard_map/reduce_scatter | solution.py:80
  28.5 34.0 %copy-start.1 = (f32[15,4,128,128]{3,2,1,0:T(8,128)}, f32[15,4,128,128]{3,2,1,0:T(8,128)S(1)}, u32[]{:S(2)}) copy-start(f32[15,4,128,128]{3,2,1,0:T(8,128)S(1)} %slice.106) | copy-start | bytes 11796484
  28.5 30.3 %copy-start.4 = (bf16[16,128,4,128]{3,2,1,0:T(4,128)(2,1)S(1)}, bf16[16,128,4,128]{3,2,1,0:T(4,128)(2,1)}, u32[]{:S(2)}) copy-start(bf16[16,128,4,128]{3,2,1,0:T(4,128)(2,1)} %reshape.95) | copy-start | bytes 6291460
  58.8 2.9 %copy-start.7 = (bf16[16,128,4,128]{3,2,1,0:T(4,128)(2,1)S(1)}, bf16[16,128,4,128]{3,2,1,0:T(4,128)(2,1)}, u32[]{:S(2)}) copy-start(bf16[16,128,4,128]{3,2,1,0:T(4,128)(2,1)} %reshape.96) | copy-start | bytes 6291460
  60.4 1.3 copy-start.14
  65.9 5.7 %copy-start.18 = (bf16[512]{0:T(512)(128)(2,1)S(1)}, bf16[512]{0:T(512)(128)(2,1)}, u32[]{:S(2)}) copy-start(bf16[512]{0:T(512)(128)(2,1)} %param.9) | copy-start | bytes 3076
  102.8 3.2 %copy-start.13 = (f32[512,2048]{1,0:T(8,128)}, f32[512,2048]{1,0:T(8,128)S(1)}, u32[]{:S(2)}) copy-start(f32[512,2048]{1,0:T(8,128)S(1)} %fusion.6) | copy-start | bytes 12582916
  116.7 4.9 %copy-start = (f32[16,128,4,128]{3,1,2,0:T(8,128)S(1)}, f32[16,128,4,128]{3,1,2,0:T(8,128)}, u32[]{:S(2)}) copy-start(f32[16,128,4,128]{3,1,2,0:T(8,128)} %get-tuple-element.19) | copy-start | bytes 12582916
  116.7 6.1 %copy-start.12 = (f32[16,128,4,128]{3,1,2,0:T(8,128)S(1)}, f32[16,128,4,128]{3,1,2,0:T(8,128)}, u32[]{:S(2)}) copy-start(f32[16,128,4,128]{3,1,2,0:T(8,128)} %copy.68) | copy-start | bytes 12582916
  122.8 2.8 %copy-start.8 = (bf16[16,128,4,128]{3,2,1,0:T(4,128)(2,1)S(1)}, bf16[16,128,4,128]{3,2,1,0:T(4,128)(2,1)}, u32[]{:S(2)}) copy-start(bf16[16,128,4,128]{3,2,1,0:T(4,128)(2,1)} %reshape.96) | copy-start | bytes 6291460
  125.6 10.3 %copy-start.10 = (bf16[16,128,4,128]{3,1,2,0:T(8,128)(2,1)}, bf16[16,128,4,128]{3,1,2,0:T(8,128)(2,1)S(1)}, u32[]{:S(2)}) copy-start(bf16[16,128,4,128]{3,1,2,0:T(8,128)(2,1)S(1)} %multiply_convert_fusion) | copy-start | bytes 6291460
  125.6 2.9 %copy-start.5 = (bf16[16,128,4,128]{3,2,1,0:T(4,128)(2,1)S(1)}, bf16[16,128,4,128]{3,2,1,0:T(4,128)(2,1)}, u32[]{:S(2)}) copy-start(bf16[16,128,4,128]{3,2,1,0:T(4,128)(2,1)} %reshape.95) | copy-start | bytes 6291460
  127.2 1.3 copy-start.16
  128.5 2.2 %copy-start.2 = (f32[15,4,128,128]{3,2,1,0:T(8,128)S(1)}, f32[15,4,128,128]{3,2,1,0:T(8,128)}, u32[]{:S(2)}) copy-start(f32[15,4,128,128]{3,2,1,0:T(8,128)} %copy-done.1) | copy-start | bytes 11796484
  158.8 29.6 %copy-start.17 = (bf16[16,4,128,128]{3,2,1,0:T(8,128)(2,1)S(1)}, bf16[16,4,128,128]{3,2,1,0:T(8,128)(2,1)}, u32[]{:S(2)}) copy-start(bf16[16,4,128,128]{3,2,1,0:T(8,128)(2,1)} %copy-done.16) | copy-start | bytes 6291460
  188.4 2.1 copy-start.3
  188.4 2.8 %copy-start.9 = (bf16[16,128,4,128]{3,2,1,0:T(4,128)(2,1)S(1)}, bf16[16,128,4,128]{3,2,1,0:T(4,128)(2,1)}, u32[]{:S(2)}) copy-start(bf16[16,128,4,128]{3,2,1,0:T(4,128)(2,1)} %reshape.96) | copy-start | bytes 6291460
  192.8 1.8 copy-start.11
  192.8 2.2 %copy-start.15 = (bf16[16,4,128,128]{3,2,1,0:T(8,128)(2,1)S(1)}, bf16[16,4,128,128]{3,2,1,0:T(8,128)(2,1)}, u32[]{:S(2)}) copy-start(bf16[16,4,128,128]{3,2,1,0:T(8,128)(2,1)} %copy-done.14) | copy-start | bytes 6291460
  195.0 1.6 copy-start.6
Sparse Core Ops, SparseCore 0:
  9.6 85.5 all-gather.3
  98.2 81.4 reduce-scatter.1
where the time goes:
time: 216 us; the launch traced here: 215 us
  local copies, waits for them, and re-layouts  74.5 us (34%)
  blocking collectives  59.1 us (27%)
  matrix products  38 us (18%)
  other arithmetic  21.5 us (10%)
  between operations  14.4 us (7%)
  waiting for transfers between devices  7.24 us (3%)
    all_gather x6, blocking collectives, prefix_by_axis(): pieces = lax.all_gather(total.astype(jnp.bfloat16), axis)  59.1 us
    unnamed x44, local copies, waits for them, and re-layouts  25.4 us
    reshape x2, local copies, waits for them, and re-layouts, on_device(): grad_heads.astype(jnp.float32).reshape(tokens, local_heads, HDIM) * scales  10.7 us
    reshape x3, local copies, waits for them, and re-layouts, split_blocks(): return array.reshape(nblocks, BLOCK, local_heads, HDIM)  10.5 us
    add x2, local copies, waits for them, and re-layouts, on_device(): attended + jnp.einsum('cshe,chef->cshf', q_blocks, prefixes, preferred_el...  10.3 us
    rev x2, local copies, waits for them, and re-layouts, on_device(): tail_sums = jnp.cumsum(block_grads[::-1], axis=0)[::-1]  10.3 us
    dot_general x1, matrix products, on_device(): jnp.dot(normed, w_slice, preferred_element_type=jnp.float32)  8.4 us
    dot_general x1, matrix products, on_device(): lax.dot_general(lax.all_gather(d_out, 'head', axis=0, tiled=True), w_slic...  7.63 us
  transfers between devices with their start and end apart: 2, of which 1 were waited for; matrix products, arithmetic and copies ran while one was open for 58% of the time, Pallas kernels for 0%

commit v1 on v0

--- a/solution.py
+++ b/solution.py
@@ -9,6 +9,11 @@
 CTX = ("ctx_0", "ctx_1", "ctx_2")
 CTX_HEAD = ("ctx_0", "ctx_1", "ctx_2", "head")
 epsilon = 1e-06
+
+
+def compute_the_fields(field_in, group_axis):
+    fresh = jnp.stack(lax.axis_size(group_axis) * [field_in], axis=0)
+    return jnp.concatenate(lax.all_to_all(fresh, group_axis, 0, 0), axis=0)
 
 
 def nothing_yet(value, identity):
@@ -84,7 +89,7 @@
         tiled=True,
     )
     grad_heads = lax.dot_general(
-        lax.all_gather(d_out, "head", axis=0, tiled=True),
+        compute_the_fields(d_out, "head"),
         w_slice,
         (((1,), (1,)), ((), ())),
         preferred_element_type=jnp.float32,

time: 216 us -> 375 us (1.74)
  waiting for transfers between devices: 7.24 us -> 153 us
  starting transfers between devices: 0.08 us -> 5.89 us
  local copies, waits for them, and re-layouts: 74.5 us -> 79.6 us
    all_to_all x0 -> x1, waiting for transfers between devices: none -> 153 us  [compute_the_fields(): return jnp.concatenate(lax.all_to_all(fresh, group_axis, 0, 0), axis=0)]
    all_gather x1 -> x0, waiting for transfers between devices: 6.54 us -> none  [on_device(): lax.all_gather(d_out, 'head', axis=0, tiled=True)]
    another operation x0 -> x1, local copies, waits for them, and re-layouts: none -> 5.9 us  [compute_the_fields(): fresh = jnp.stack(lax.axis_size(group_axis) * [field_in], axis=0)]
    all_to_all x0 -> x1, starting transfers between devices: none -> 5.85 us  [compute_the_fields(): return jnp.concatenate(lax.all_to_all(fresh, group_axis, 0, 0), axis=0)]
    unnamed x44 -> x48, local copies, waits for them, and re-layouts: 25.4 us -> 24.3 us
  transfers between devices with their start and end apart: 2 -> 2, of which waited for: 1 -> 1; matrix products, arithmetic and copies ran while one was open for 58% -> 23% of each run, Pallas kernels for 0% -> 0%
where the time goes in v1:
time: 375 us; the launch traced here: 374 us
  waiting for transfers between devices  153 us (41%)
  local copies, waits for them, and re-layouts  79.6 us (21%)
  blocking collectives  58.8 us (16%)
  matrix products  40.8 us (11%)
  other arithmetic  21.2 us (6%)
  between operations  14.4 us (4%)
  starting transfers between devices  5.89 us (2%)
    all_to_all x1, waiting for transfers between devices, compute_the_fields(): return jnp.concatenate(lax.all_to_all(fresh, group_axis, 0, 0), axis=0)  153 us
    all_gather x6, blocking collectives, prefix_by_axis(): pieces = lax.all_gather(total.astype(jnp.bfloat16), axis)  58.8 us
    unnamed x48, local copies, waits for them, and re-layouts  24.3 us
    reshape x2, local copies, waits for them, and re-layouts, on_device(): grad_heads.astype(jnp.float32).reshape(tokens, local_heads, HDIM) * scales  10.6 us
    add x2, local copies, waits for them, and re-layouts, on_device(): attended + jnp.einsum('cshe,chef->cshf', q_blocks, prefixes, preferred_el...  10.1 us
    rev x2, local copies, waits for them, and re-layouts, on_device(): tail_sums = jnp.cumsum(block_grads[::-1], axis=0)[::-1]  9.99 us
    reshape x3, local copies, waits for them, and re-layouts, split_blocks(): return array.reshape(nblocks, BLOCK, local_heads, HDIM)  9.44 us
    dot_general x1, matrix products, on_device(): jnp.dot(normed, w_slice, preferred_element_type=jnp.float32)  8.37 us
  transfers between devices with their start and end apart: 2, of which 1 were waited for; matrix products, arithmetic and copies ran while one was open for 23% of the time, Pallas kernels for 0%

profile of v1, /device:TPU:0, one launch (start us, length us, event | category | flops | bytes accessed | tf_op | source)
XLA Modules:
  0.0 373.9 jit_solution(15603049400353060921)
XLA Ops:
  7.3 2.6 reshape.101
  9.8 4.3 %reshape.100 = bf16[16,128,4,128]{3,2,1,0:T(4,128)(2,1)} reshape(bf16[2048,512]{1,0:T(8,128)(2,1)} %param.7) | data formatting | bytes 4194304 | tf_op jit(solution)/shard_map/reshape | solution.py:57
  16.7 6.4 %fusion.63 = f32[16,4,128,128]{3,2,1,0:T(8,128)S(1)} fusion(f32[16,4,128,128]{3,2,1,0:T(8,128)S(1)} %get-tuple-element.17), kind=kOutput, calls=%fused_computation.101 | output fusion | flops 15728640 | bytes 8388608 | tf_op jit(solution)/shard_map/jit(cumsum)/reduce_window_sum | solution.py:72
  27.6 14.1 %all_gather.25 = bf16[4,4,128,128]{3,2,1,0:T(8,128)(2,1)S(1)} all-gather(bf16[1,4,128,128]{3,2,1,0:T(8,128)(2,1)S(1)} %fusion.52), channel_id=1, replica_groups=mesh['ctx_0'=4,'ctx_1'=4,'ctx_2'=2,'head'=4] {'ctx_1'}, dimensions={0}, use_global_device_ids=true | all-gather | bytes 655360 | tf_op jit(solution)/shard_map/all_gather | solution.py:28
  41.8 14.3 %all_gather.26 = bf16[4,4,128,128]{3,2,1,0:T(8,128)(2,1)} all-gather(bf16[1,4,128,128]{3,2,1,0:T(8,128)(2,1)S(1)} %fusion.51), channel_id=1, replica_groups=mesh['ctx_0'=4,'ctx_1'=4,'ctx_2'=2,'head'=4] {'ctx_0'}, dimensions={0}, use_global_device_ids=true | all-gather | bytes 655360 | tf_op jit(solution)/shard_map/all_gather | solution.py:28
  56.0 2.5 reshape.99
  58.6 3.3 select_convert_fusion.1
  65.0 3.5 multiply_reduce_fusion
  68.4 5.5 %copy.66 = f32[16,128,4,128]{1,0,3,2:T(8,128)} copy(f32[16,128,4,128]{3,1,2,0:T(8,128)} %get-tuple-element.19) | data formatting | bytes 8388608 | tf_op jit(solution)/shard_map/add | solution.py:76
  74.0 4.0 %fusion.1 = bf16[2048,512]{0,1:T(8,128)(2,1)S(1)} fusion(f32[64,8,16,128]{3,2,1,0:T(8,128)} %bitcast.94, f32[2048,4]{0,1:T(4,128)S(1)} %get-tuple-element.13, f32[512]{0:T(512)S(1)} %get-tuple-element.15), kind=kLoop, calls=%fused_computation.3 | loop fusion | flops 3145728 | bytes 6326272 | tf_op jit(solution)/shard_map/convert_element_type | solution.py:83
  77.9 8.4 %convolution_convert_fusion = bf16[2048,2048]{1,0:T(8,128)(2,1)} fusion(bf16[2048,512]{0,1:T(8,128)(2,1)S(1)} %fusion.1, bf16[2048,2048]{1,0:T(8,128)(2,1)} %param.10, s32[]{:T(128)S(6)} %select_n.175), kind=kOutput, calls=%fused_computation | convolution fusion | flops 4299161600 | bytes 12582916 | tf_op jit(solution)/shard_map/dot_general | solution.py:86
  86.3 5.9 %stack.2 = bf16[4,512,2048]{2,1,0:T(8,128)(2,1)} broadcast(bf16[512,2048]{1,0:T(8,128)(2,1)} %param.11), dimensions={1,2} | broadcast | bytes 10485760 | tf_op jit(solution)/shard_map/stack | solution.py:15
  92.2 5.9 %all-to-all-start = ((bf16[4,512,2048]{2,1,0:T(8,128)(2,1)}), bf16[4,512,2048]{2,1,0:T(8,128)(2,1)}, u32[]{:S(2)}, u32[]{:S(2)}) async-start(bf16[4,512,2048]{2,1,0:T(8,128)(2,1)} %stack.2), calls=%async_computation.1 | async-start | bytes 16777216 | tf_op jit(solution)/shard_map/all_to_all | solution.py:16
  98.1 4.6 %copy.70 = f32[16,128,4,128]{3,1,0,2:T(8,128)} copy(f32[16,128,4,128]{3,1,2,0:T(8,128)} %get-tuple-element.19) | data formatting | bytes 8388608 | tf_op jit(solution)/shard_map/add | solution.py:76
  102.7 153.0 %all-to-all-done = bf16[4,512,2048]{2,1,0:T(8,128)(2,1)} async-done(((bf16[4,512,2048]{2,1,0:T(8,128)(2,1)}), bf16[4,512,2048]{2,1,0:T(8,128)(2,1)}, u32[]{:S(2)}, u32[]{:S(2)}) %all-to-all-start) | async-done | bytes 8388640 | tf_op jit(solution)/shard_map/all_to_all | solution.py:16
  255.7 7.6 %fusion.6 = f32[512,2048]{1,0:T(8,128)S(1)} fusion(bf16[2048,2048]{1,0:T(8,128)(2,1)} %bitcast.7, bf16[2048,2048]{1,0:T(8,128)(2,1)} %param.10, s32[]{:T(128)S(6)} %select_n.175), kind=kOutput, calls=%fused_computation.20 | convolution fusion | flops 4297064448 | bytes 14680068 | tf_op jit(solution)/shard_map/dot_general | solution.py:91
  263.4 3.2 copy.106
  266.6 5.2 %copy.68 = f32[16,128,4,128]{3,1,2,0:T(8,128)} copy(f32[16,128,4,128]{1,0,3,2:T(8,128)} %bitcast.97) | data formatting | bytes 8388608 | tf_op jit(solution)/shard_map/reshape | solution.py:97
  271.8 5.3 %copy.69 = f32[2048,4,128]{2,0,1:T(8,128)} copy(f32[2048,4,128]{0,2,1:T(8,128)} %bitcast.96) | data formatting | bytes 8388608 | tf_op jit(solution)/shard_map/reshape | solution.py:97
  277.2 4.8 %fusion.5 = f32[2048,4]{0,1:T(4,128)S(1)} fusion(f32[16,128,4,128]{3,1,0,2:T(8,128)} %copy.70, f32[2048,4,128]{2,0,1:T(8,128)} %copy.69, f32[4,128]{1,0:T(4,128)S(1)} %get-tuple-element.14, f32[2048,4]{0,1:T(4,128)S(1)} %get-tuple-element.13), kind=kLoop, calls=%fused_computation.10 | loop fusion | flops 4186112 | bytes 8456192 | tf_op jit(solution)/shard_map/reduce_sum | solution.py:99
  283.1 2.5 multiply_convert_fusion
  295.8 2.9 fusion.62
  298.8 4.6 %rev.4 = f32[16,4,128,128]{2,3,1,0:T(8,128)} reverse(f32[16,4,128,128]{2,3,1,0:T(8,128)} %get-tuple-element.21), dimensions={0} | reverse | bytes 8388608 | tf_op jit(solution)/shard_map/rev | solution.py:109
  303.4 5.3 %copy.81 = f32[16,4,128,128]{3,2,1,0:T(8,128)} copy(f32[16,4,128,128]{2,3,1,0:T(8,128)} %rev.4) | data formatting | bytes 8388608 | tf_op jit(solution)/shard_map/rev | solution.py:109
  308.7 2.7 fusion.64
  313.8 4.4 %slice.91 = f32[15,4,128,128]{3,2,1,0:T(8,128)} reverse(f32[15,4,128,128]{3,2,1,0:T(8,128)} %slice.117), dimensions={0} | reverse | bytes 7864320 | tf_op jit(solution)/shard_map/slice | solution.py:110
  320.6 13.4 %all_gather.28 = bf16[4,4,128,128]{3,2,1,0:T(8,128)(2,1)S(1)} all-gather(bf16[1,4,128,128]{3,2,1,0:T(8,128)(2,1)S(1)} %fusion.53), channel_id=1, replica_groups=mesh['ctx_0'=4,'ctx_1'=4,'ctx_2'=2,'head'=4] {'ctx_1'}, dimensions={0}, use_global_device_ids=true | all-gather | bytes 655360 | tf_op jit(solution)/shard_map/all_gather | solution.py:28
  334.1 12.9 %all_gather.29 = bf16[4,4,128,128]{3,2,1,0:T(8,128)(2,1)S(1)} all-gather(bf16[1,4,128,128]{3,2,1,0:T(8,128)(2,1)S(1)} %fusion.50), channel_id=1, replica_groups=mesh['ctx_0'=4,'ctx_1'=4,'ctx_2'=2,'head'=4] {'ctx_0'}, dimensions={0}, use_global_device_ids=true | all-gather | bytes 655360 | tf_op jit(solution)/shard_map/all_gather | solution.py:28
  350.1 2.9 fusion.9
  353.0 4.3 %copy.100 = bf16[16,128,4,128]{3,2,1,0:T(4,128)(2,1)} copy(bf16[16,128,4,128]{1,3,2,0:T(8,128)(2,1)} %fusion.9) | data formatting | bytes 4194304
  357.3 2.6 fusion.22
  364.1 3.0 copy_bitcast_fusion
  (70 shorter events, 33.3 us)
Async XLA Ops:
  7.2 359.9 %reduce-scatter.2.cloned.1.call-start = ((), (), s32[]{:S(2)}) async-start(), calls=%async_computation.2 | async-start | bytes 10485760 | tf_op jit(solution)/shard_map/reduce_scatter | solution.py:85
  9.8 4.4 %copy-start.5 = (bf16[16,128,4,128]{3,2,1,0:T(4,128)(2,1)}, bf16[16,128,4,128]{3,2,1,0:T(4,128)(2,1)S(1)}, u32[]{:S(2)}) copy-start(bf16[16,128,4,128]{3,2,1,0:T(4,128)(2,1)S(1)} %reshape.101) | copy-start | bytes 6291460
  58.6 3.3 copy-start.6
  61.9 1.3 copy-start.16
  61.9 1.4 copy-start.19
  61.9 3.0 copy-start.1
  68.4 5.5 %copy-start.20 = (bf16[512]{0:T(512)(128)(2,1)S(1)}, bf16[512]{0:T(512)(128)(2,1)}, u32[]{:S(2)}) copy-start(bf16[512]{0:T(512)(128)(2,1)} %param.9) | copy-start | bytes 3076
  92.2 163.5 %all-to-all-start = ((bf16[4,512,2048]{2,1,0:T(8,128)(2,1)}), bf16[4,512,2048]{2,1,0:T(8,128)(2,1)}, u32[]{:S(2)}, u32[]{:S(2)}) async-start(bf16[4,512,2048]{2,1,0:T(8,128)(2,1)} %stack.2), calls=%async_computation.1 | async-start | bytes 16777216 | tf_op jit(solution)/shard_map/all_to_all | solution.py:16
  263.4 3.2 copy-start.14
  277.2 4.8 %copy-start = (f32[16,128,4,128]{3,1,2,0:T(8,128)S(1)}, f32[16,128,4,128]{3,1,2,0:T(8,128)}, u32[]{:S(2)}) copy-start(f32[16,128,4,128]{3,1,2,0:T(8,128)} %get-tuple-element.19) | copy-start | bytes 12582916
  277.2 5.9 %copy-start.13 = (f32[16,128,4,128]{3,1,2,0:T(8,128)S(1)}, f32[16,128,4,128]{3,1,2,0:T(8,128)}, u32[]{:S(2)}) copy-start(f32[16,128,4,128]{3,1,2,0:T(8,128)} %copy.68) | copy-start | bytes 12582916
  283.1 2.5 copy-start.7
  285.6 10.2 %copy-start.11 = (bf16[16,128,4,128]{3,1,2,0:T(8,128)(2,1)}, bf16[16,128,4,128]{3,1,2,0:T(8,128)(2,1)S(1)}, u32[]{:S(2)}) copy-start(bf16[16,128,4,128]{3,1,2,0:T(8,128)(2,1)S(1)} %multiply_convert_fusion) | copy-start | bytes 6291460
  285.6 2.9 copy-start.9
  287.2 1.3 copy-start.18
  288.6 2.1 copy-start.2
  318.4 28.9 %copy-start.12 = (bf16[16,128,4,128]{3,1,2,0:T(8,128)(2,1)S(1)}, bf16[16,128,4,128]{3,1,2,0:T(8,128)(2,1)}, u32[]{:S(2)}) copy-start(bf16[16,128,4,128]{3,1,2,0:T(8,128)(2,1)} %copy-done.11) | copy-start | bytes 6291460
  318.4 28.9 %copy-start.17 = (bf16[16,4,128,128]{3,2,1,0:T(8,128)(2,1)S(1)}, bf16[16,4,128,128]{3,2,1,0:T(8,128)(2,1)}, u32[]{:S(2)}) copy-start(bf16[16,4,128,128]{3,2,1,0:T(8,128)(2,1)} %copy-done.16) | copy-start | bytes 6291460
  347.3 2.1 copy-start.3
  347.3 2.8 copy-start.10
  357.3 2.7 copy-start.4
  357.3 3.4 copy-start.8
  362.3 1.8 copy-start.15
Sparse Core Ops, SparseCore 0:
  86.4 147.3 reduce-scatter.1
